TPU v7x, 32 devices: a whole 2x2x4 slice. The times are simulated.
32 devices in a mesh: row: 4 (over x, core), col: 8 (over z, y).
Axes of the slice: x: 2, y: 2, z: 4, core: 2. Of those that a mesh axis runs over, the one named last changes fastest.
Arguments:
- rhs_c: float32 [12, 512, 6, 1024], P(None, 'row', None, 'col'), may hold values from -6 to 6
- rhs_f: float32 [12, 512, 6, 1024], P(None, 'row', None, 'col'), may hold values from -6 to 6
- pencil_a: bfloat16 [12, 512, 6, 1024], P(None, 'row', None, 'col'), may hold values from -0.5 to 0.5
- pencil_d: bfloat16 [12, 512, 6, 1024], P(None, 'row', None, 'col'), may hold values from -0.5 to 0.5
- pencil_b: bfloat16 [12, 512, 6, 1024], P(None, 'row', None, 'col'), may hold values from -0.5 to 0.5
- pencil_e: bfloat16 [12, 512, 6, 1024], P(None, 'row', None, 'col'), may hold values from -0.5 to 0.5
- d_inverse: float32 [12, 512, 128], P(None, 'row'), may hold values from -0.25 to 2.5
- left_vectors: float32 [12, 512, 128], P(None, 'row'), may hold values from -0.25 to 2.5
- left_inverse: float32 [12, 512, 128], P(None, 'row'), may hold values from -0.25 to 2.5
- left_eigs: float32 [12, 512], P(None, 'row'), may hold values from 1 to 3
- e_inverse: float32 [6, 1024, 128], P(None, 'col'), may hold values from -0.25 to 2.5
- right_vectors: float32 [6, 1024, 128], P(None, 'col'), may hold values from -0.25 to 2.5
- right_inverse: float32 [6, 1024, 128], P(None, 'col'), may hold values from -0.25 to 2.5
- right_eigs: float32 [6, 1024], P(None, 'col'), may hold values from -3 to -1
Outputs:
- updated_c: float32 [12, 512, 6, 1024], P(None, 'row', None, 'col')
- updated_f: float32 [12, 512, 6, 1024], P(None, 'row', None, 'col')
- solved_r: float32 [12, 512, 6, 1024], P(None, 'row', None, 'col')
- solved_l: float32 [12, 512, 6, 1024], P(None, 'row', None, 'col')
All inputs are finite; a program needn't handle non-finite values.
Results may differ from a plain program's by a relative error of at most 0.0003.
Values may be sent and summed in bfloat16 or wider, within the bound.
A program may use at most 128 MiB of HBM per device.

v0:
```python
import jax
import jax.numpy as jnp
from jax import lax
from jax.sharding import PartitionSpec as P

TILE = 128
ORDER = 6144
STEPS = 3


def padded(value, sides, width):
    for axis, dim in sides:
        devices, length = (lax.axis_size(axis), value.shape[dim])
        up = [(i, (i + 1) % devices) for i in range(devices)]
        down = [(j, i) for i, j in up]
        last = lax.slice_in_dim(value, length - width, length, axis=dim)
        initial = lax.slice_in_dim(value, 0, width, axis=dim)
        before = lax.ppermute(last, axis, up)
        after = lax.ppermute(initial, axis, down)
        value = jnp.concatenate([before, value, after], axis=dim)
    return value


def product(left, right):
    return jnp.einsum("bij,bjk->bik", left, right, precision=lax.Precision.HIGHEST)


def solve_tiles(
    a_diag,
    e_diag,
    resid_c,
    resid_f,
    inv_d,
    vec_left,
    back_left,
    eig_left,
    inv_e,
    vec_right,
    back_right,
    eig_right,
):
    coupled = product(a_diag, inv_d)
    merged = product(resid_c - product(coupled, resid_f), inv_e)
    spectral = product(product(back_left, merged), vec_right)
    spectral = spectral / (eig_left[:, :, None] - eig_right[:, None, :])
    new_l = product(product(vec_left, spectral), back_right)
    new_r = product(inv_d, resid_f + product(new_l, e_diag))
    return (new_r, new_l)


def body(
    rhs_c,
    rhs_f,
    pencil_a,
    pencil_d,
    pencil_b,
    pencil_e,
    d_inverse,
    left_vectors,
    left_inverse,
    left_eigs,
    e_inverse,
    right_vectors,
    right_inverse,
    right_eigs,
):
    highest = lax.Precision.HIGHEST
    count_rows = lax.axis_size("row")
    count_cols = lax.axis_size("col")
    this_row = lax.axis_index("row")
    this_col = lax.axis_index("col")
    rows_dev = rhs_c.shape[0]
    cols_dev = rhs_c.shape[2]
    blocks = ORDER // TILE
    local_rows = jnp.arange(rows_dev, dtype=jnp.int32)
    local_cols = jnp.arange(cols_dev, dtype=jnp.int32)
    block_rows = local_rows * count_rows + this_row
    block_cols = local_cols * count_cols + this_col
    near_ad = padded(jnp.stack([pencil_a, pencil_d]), (("col", 4),), TILE)
    near_ad = near_ad.reshape(2, rows_dev, TILE, cols_dev, 3, TILE)
    near_be = padded(jnp.stack([pencil_b, pencil_e]), (("row", 2),), TILE)
    near_be = near_be.reshape(2, rows_dev, 3, TILE, cols_dev, TILE)
    current_c = rhs_c
    current_f = rhs_f
    out_r = jnp.zeros_like(rhs_c)
    out_l = jnp.zeros_like(rhs_c)
    for step in range(STEPS):
        offset = 1 - step
        front_rows = block_cols + offset
        col_valid = (front_rows >= 0) & (front_rows < blocks)
        rows_clip = jnp.clip(front_rows, 0, blocks - 1)
        front_cols = block_rows - offset
        row_valid = (front_cols >= 0) & (front_cols < blocks)
        cols_clip = jnp.clip(front_cols, 0, blocks - 1)
        slot_cols = jnp.clip(rows_clip // count_cols, 0, cols_dev - 1)
        picked_ad = jnp.take(near_ad[:, :, :, :, 1 + offset, :], slot_cols, axis=3)
        panel_a = picked_ad[0]
        panel_d = picked_ad[1]
        slot_rows = jnp.clip(cols_clip // count_rows, 0, rows_dev - 1)
        picked_be = jnp.take(near_be[:, :, 1 - offset, :, :, :], slot_rows, axis=1)
        panel_b = picked_be[0]
        panel_e = picked_be[1]
        owned = col_valid & (rows_clip % count_rows == this_row)
        own_slot = jnp.clip(rows_clip // count_rows, 0, rows_dev - 1)
        resid_c = current_c[own_slot, :, local_cols, :]
        resid_f = current_f[own_slot, :, local_cols, :]
        a_diag = panel_a[own_slot, :, local_cols, :].astype(jnp.float32)
        e_diag = panel_e[own_slot, :, local_cols, :].astype(jnp.float32)
        new_r, new_l = solve_tiles(
            a_diag,
            e_diag,
            resid_c,
            resid_f,
            d_inverse[own_slot],
            left_vectors[own_slot],
            left_inverse[own_slot],
            left_eigs[own_slot],
            e_inverse,
            right_vectors,
            right_inverse,
            right_eigs,
        )
        new_r = jnp.where(owned[:, None, None], new_r, 0.0)
        new_l = jnp.where(owned[:, None, None], new_l, 0.0)
        l_slot = jnp.clip(cols_clip // count_cols, 0, cols_dev - 1)
        front_r = lax.psum(new_r, "row")
        picked = jnp.where((cols_clip % count_cols == this_col)[:, None, None], new_l[l_slot], 0.0)
        front_l = lax.psum(picked, "col")
        front_r = jnp.where(col_valid[:, None, None], front_r, 0.0)
        front_l = jnp.where(row_valid[:, None, None], front_l, 0.0)
        mask_a = (block_rows[:, None] < front_rows[None, :]) & col_valid[None, :]
        term_c = jnp.einsum(
            "apbq,bqs->apbs", panel_a.astype(jnp.float32), front_r, precision=highest
        )
        term_f = jnp.einsum(
            "apbq,bqs->apbs", panel_d.astype(jnp.float32), front_r, precision=highest
        )
        mask_b = (block_cols[None, :] > front_cols[:, None]) & row_valid[:, None]
        gain_c = jnp.einsum(
            "apq,aqbs->apbs", front_l, panel_b.astype(jnp.float32), precision=highest
        )
        gain_f = jnp.einsum(
            "apq,aqbs->apbs", front_l, panel_e.astype(jnp.float32), precision=highest
        )
        wide_a = mask_a[:, None, :, None]
        wide_b = mask_b[:, None, :, None]
        current_c = current_c - jnp.where(wide_a, term_c, 0.0) + jnp.where(wide_b, gain_c, 0.0)
        current_f = current_f - jnp.where(wide_a, term_f, 0.0) + jnp.where(wide_b, gain_f, 0.0)
        place = (owned[None, :] & (local_rows[:, None] == own_slot[None, :]))[:, None, :, None]
        out_r = out_r + jnp.where(place, new_r.transpose(1, 0, 2)[None], 0.0)
        out_l = out_l + jnp.where(place, new_l.transpose(1, 0, 2)[None], 0.0)
    return (current_c, current_f, out_r, out_l)


def solution(mesh):
    in_specs = (
        P(None, "row", None, "col"),
        P(None, "row", None, "col"),
        P(None, "row", None, "col"),
        P(None, "row", None, "col"),
        P(None, "row", None, "col"),
        P(None, "row", None, "col"),
        P(None, "row", None),
        P(None, "row", None),
        P(None, "row", None),
        P(None, "row"),
        P(None, "col", None),
        P(None, "col", None),
        P(None, "col", None),
        P(None, "col"),
    )
    out_specs = (
        P(None, "row", None, "col"),
        P(None, "row", None, "col"),
        P(None, "row", None, "col"),
        P(None, "row", None, "col"),
    )
    return jax.shard_map(body, mesh=mesh, in_specs=in_specs, out_specs=out_specs, check_vma=False)
```

profile of v0, /device:TPU:0, one launch (start us, length us, event | category | flops | bytes accessed | tf_op | source)
XLA Modules:
  0.0 719.9 jit_solution(12369988336342731525)
XLA Ops:
  32.4 6.0 copy.88
  45.1 6.1 copy.91
  88.0 136.5 %collective-permute-done = bf16[2,12,128,6,128]{2,4,3,1,0:T(8,128)(2,1)} collective-permute-done((bf16[2,12,128,6,128]{2,4,3,1,0:T(8,128)(2,1)}, bf16[2,12,128,6,128]{2,4,3,1,0:T(8,128)(2,1)}, u32[]{:S(2)}, u32[]{:S(2)}) %collective-permute-start) | collective-permute-done | bytes 4718624 | tf_op jit(solution)/shard_map/ppermute | solution.py:18
  226.7 6.9 pad_maximum_fusion
  233.7 6.2 fusion.108
  239.9 6.6 copy.83
  246.5 5.8 gather_fusion.27
  272.5 6.9 pad_maximum_fusion.1
  279.5 6.4 slice_bitcast_fusion
  285.9 6.0 gather_fusion.28
  302.4 6.6 copy.93
  309.0 6.0 gather_fusion.29
  320.4 6.7 copy.106
  327.1 5.9 gather_fusion.30
  338.2 6.0 gather_fusion.32
  356.4 5.9 gather_fusion.31
  372.9 14.3 %all-reduce.7.cloned.1.call-done = f32[6,128,128]{2,1,0:T(8,128)} async-done(((f32[6,128,128]{2,1,0:T(8,128)}), f32[6,128,128]{2,1,0:T(8,128)}) %all-reduce.7.cloned.1.call-update) | async-done | bytes 393232 | tf_op jit(solution)/shard_map/psum | solution.py:126
  387.3 10.1 %fusion.11 = f32[12,128,6,128]{1,3,0,2:T(8,128)} fusion(f32[12,128,6,128]{1,3,0,2:T(8,128)} %copy.88, f32[12,128,6,128]{1,3,0,2:T(8,128)} %fusion.31, pred[12,6]{0,1:T(8,128)(4,1)S(1)} %copy-done.48, pred[12,6]{0,1:T(8,128)(4,1)S(1)} %copy-done.49, f32[6,128,128]{2,1,0:T(8,128)} %all-reduce.7.cloned.1.call-done, pred[6]{0:T(512)(128)(4,1)S(1)} %copy-done.65, ...), kind=kOutput, calls=%fused_computation.57 | convolution fusion | flops 1816756224 | bytes 16908438 | tf_op jit(solution)/shard_map/apbq,bqs->apbs/dot_general | solution.py:132
  404.9 7.1 fusion.9
  442.9 55.0 %all-reduce.13.cloned.1.call-done = f32[12,128,128]{2,1,0:T(8,128)} async-done(((f32[12,128,128]{2,1,0:T(8,128)}), f32[12,128,128]{2,1,0:T(8,128)}) %all-reduce.13.cloned.1.call-update) | async-done | bytes 786448 | tf_op jit(solution)/shard_map/psum | solution.py:128
  503.3 29.3 %all-reduce.11.cloned.1.call-done = f32[6,128,128]{2,1,0:T(8,128)} async-done(((f32[6,128,128]{2,1,0:T(8,128)}), f32[6,128,128]{2,1,0:T(8,128)}) %all-reduce.11.cloned.1.call-update) | async-done | bytes 393232 | tf_op jit(solution)/shard_map/psum | solution.py:126
  532.7 10.2 %fusion.7 = f32[12,128,6,128]{1,3,0,2:T(8,128)} fusion(f32[12,128,6,128]{1,3,0,2:T(8,128)} %fusion.11, f32[12,128,6,128]{1,3,0,2:T(8,128)} %fusion.27, pred[12,6]{0,1:T(8,128)(4,1)S(1)} %copy-done.47, pred[12,6]{0,1:T(8,128)(4,1)S(1)} %copy-done.46, f32[6,128,128]{2,1,0:T(8,128)} %all-reduce.11.cloned.1.call-done, pred[6]{0:T(512)(128)(4,1)} %copy-done.50, ...), kind=kOutput, calls=%fused_computation.51 | convolution fusion | flops 1816756224 | bytes 16908944 | tf_op jit(solution)/shard_map/apbq,bqs->apbs/dot_general | solution.py:132
  550.4 7.2 %fusion.5 = f32[12,128,6,128]{1,3,0,2:T(8,128)} fusion(f32[12,128,6,128]{1,3,0,2:T(8,128)} %fusion.9, f32[12,128,6,128]{1,3,0,2:T(8,128)S(1)} %fusion.25, pred[12,6]{0,1:T(8,128)(4,1)S(1)} %copy-done.47, pred[12,6]{0,1:T(8,128)(4,1)S(1)} %copy-done.46, bf16[2,12,128,6,128]{4,2,1,3,0:T(8,128)(2,1)S(1)} %bitcast.225, f32[6,128,128]{2,1,0:T(8,128)S(1)} %copy-done.40, ...), kind=kOutput, calls=%fused_computation.48 | convolution fusion | flops 1816756224 | bytes 16910848 | tf_op jit(solution)/shard_map/apbq,bqs->apbs/dot_general | solution.py:135
  572.0 6.3 select_add_fusion
  578.3 6.1 copy.127
  584.4 6.2 copy.128
  590.7 53.6 %all-reduce.17.cloned.1.call-done = f32[12,128,128]{2,1,0:T(8,128)} async-done(((f32[12,128,128]{2,1,0:T(8,128)}), f32[12,128,128]{2,1,0:T(8,128)}) %all-reduce.17.cloned.1.call-update) | async-done | bytes 786448 | tf_op jit(solution)/shard_map/psum | solution.py:128
  649.5 28.9 %all-reduce.15.cloned.1.call-done = f32[6,128,128]{2,1,0:T(8,128)} async-done(((f32[6,128,128]{2,1,0:T(8,128)}), f32[6,128,128]{2,1,0:T(8,128)}) %all-reduce.15.cloned.1.call-update) | async-done | bytes 393232 | tf_op jit(solution)/shard_map/psum | solution.py:126
  678.4 10.1 %fusion.1 = f32[12,128,6,128]{1,3,0,2:T(8,128)} fusion(f32[12,128,6,128]{1,3,0,2:T(8,128)} %fusion.5, f32[12,128,6,128]{1,3,0,2:T(8,128)} %fusion.21, pred[12,6]{0,1:T(8,128)(4,1)S(1)} %copy-done.45, pred[12,6]{0,1:T(8,128)(4,1)S(1)} %get-tuple-element.34, bf16[2,12,128,6,128]{4,2,1,3,0:T(8,128)(2,1)} %fusion.13, ...), kind=kOutput, calls=%fused_computation.42 | convolution fusion | flops 1816756224 | bytes 16908438 | tf_op jit(solution)/shard_map/apbq,bqs->apbs/dot_general | solution.py:135
  688.5 6.5 copy.126
  697.7 8.8 %fusion.3 = f32[12,128,6,128]{1,3,0,2:T(8,128)} fusion(f32[12,128,6,128]{1,3,0,2:T(8,128)} %fusion.7, f32[12,128,6,128]{1,3,0,2:T(8,128)S(1)} %fusion.23, pred[12,6]{0,1:T(8,128)(4,1)S(1)} %copy-done.45, pred[12,6]{0,1:T(8,128)(4,1)S(1)} %get-tuple-element.34, f32[6,128,128]{2,1,0:T(8,128)S(1)} %copy-done.41, pred[6]{0:T(512)(128)(4,1)S(1)} %copy-done.61, ...), kind=kOutput, calls=%fused_computation.45 | convolution fusion | flops 1816756224 | bytes 16908438 | tf_op jit(solution)/shard_map/apbq,bqs->apbs/dot_general | solution.py:132
  706.5 6.0 copy.125
  (321 shorter events, 207.4 us)
Async XLA Ops:
  7.2 44.0 %copy-start = (f32[12,128,128]{2,1,0:T(8,128)S(1)}, f32[12,128,128]{2,1,0:T(8,128)}, u32[]{:S(2)}) copy-start(f32[12,128,128]{2,1,0:T(8,128)} %param.24) | copy-start | bytes 2359300
  7.2 360.5 %all-reduce.9.cloned.1.call-start = ((), (), s32[]{:S(2)}) async-start(), calls=%async_computation.1 | async-start | bytes 1572864 | tf_op jit(solution)/shard_map/psum | solution.py:128
  19.0 205.5 %collective-permute-start = (bf16[2,12,128,6,128]{2,4,3,1,0:T(8,128)(2,1)}, bf16[2,12,128,6,128]{2,4,3,1,0:T(8,128)(2,1)}, u32[]{:S(2)}, u32[]{:S(2)}) collective-permute-start(bf16[2,12,128,6,128]{2,4,3,1,0:T(8,128)(2,1)} %pad_maximum_fusion.2), channel_id=1, source_target_pairs={{0,1},{1,2},{2,3},{3,4},{4,5},{5,6},{6,7},{7,0},{8,9},{9,10},{10,1... | collective-permute-start | bytes 14155784 | tf_op jit(solution)/shard_map/ppermute | solution.py:18
  22.0 204.7 %collective-permute-start.1 = (bf16[2,12,128,6,128]{2,4,3,1,0:T(8,128)(2,1)}, bf16[2,12,128,6,128]{2,4,3,1,0:T(8,128)(2,1)}, u32[]{:S(2)}, u32[]{:S(2)}) collective-permute-start(bf16[2,12,128,6,128]{2,4,3,1,0:T(8,128)(2,1)} %pad_maximum_fusion.2), channel_id=1, source_target_pairs={{1,0},{2,1},{3,2},{4,3},{5,4},{6,5},{7,6},{0,7},{9,8},{10,9},{11,1... | collective-permute-start | bytes 14155784 | tf_op jit(solution)/shard_map/ppermute | solution.py:19
  27.7 244.8 %collective-permute-start.2 = (bf16[2,12,128,6,128]{4,2,3,1,0:T(8,128)(2,1)}, bf16[2,12,128,6,128]{4,2,3,1,0:T(8,128)(2,1)}, u32[]{:S(2)}, u32[]{:S(2)}) collective-permute-start(bf16[2,12,128,6,128]{4,2,3,1,0:T(8,128)(2,1)} %pad_maximum_fusion.3), channel_id=1, source_target_pairs={{0,8},{8,16},{16,24},{24,0},{1,9},{9,17},{17,25},{25,1},{2,10},{10... | collective-permute-start | bytes 14155784 | tf_op jit(solution)/shard_map/ppermute | solution.py:18
  27.7 244.8 %collective-permute-start.3 = (bf16[2,12,128,6,128]{4,2,3,1,0:T(8,128)(2,1)}, bf16[2,12,128,6,128]{4,2,3,1,0:T(8,128)(2,1)}, u32[]{:S(2)}, u32[]{:S(2)}) collective-permute-start(bf16[2,12,128,6,128]{4,2,3,1,0:T(8,128)(2,1)} %pad_maximum_fusion.3), channel_id=1, source_target_pairs={{8,0},{16,8},{24,16},{0,24},{9,1},{17,9},{25,17},{1,25},{10,2},{18... | collective-permute-start | bytes 14155784 | tf_op jit(solution)/shard_map/ppermute | solution.py:19
  45.1 14.2 %copy-start.42 = (f32[12,128]{1,0:T(8,128)S(1)}, f32[12,128]{1,0:T(8,128)}, u32[]{:S(2)}) copy-start(f32[12,128]{1,0:T(8,128)} %param.27) | copy-start | bytes 18436
  76.0 157.6 %copy-start.66 = (pred[12]{0:T(512)(128)(4,1)}, pred[12]{0:T(512)(128)(4,1)S(1)}, u32[]{:S(2)}) copy-start(pred[12]{0:T(512)(128)(4,1)S(1)} %compare_and_fusion.18) | copy-start | bytes 40
  76.0 157.6 %copy-start.64 = (pred[6]{0:T(512)(128)(4,1)}, pred[6]{0:T(512)(128)(4,1)S(1)}, u32[]{:S(2)}) copy-start(pred[6]{0:T(512)(128)(4,1)S(1)} %compare_and_fusion.20) | copy-start | bytes 22
  78.3 155.3 %copy-start.56 = (pred[6]{0:T(512)(128)(4,1)}, pred[6]{0:T(512)(128)(4,1)S(1)}, u32[]{:S(2)}) copy-start(pred[6]{0:T(512)(128)(4,1)S(1)} %get-tuple-element.55) | copy-start | bytes 22
  78.4 155.3 %copy-start.50 = (pred[6]{0:T(512)(128)(4,1)}, pred[6]{0:T(512)(128)(4,1)S(1)}, u32[]{:S(2)}) copy-start(pred[6]{0:T(512)(128)(4,1)S(1)} %get-tuple-element.57) | copy-start | bytes 22
  78.4 155.3 %copy-start.54 = (pred[6]{0:T(512)(128)(4,1)}, pred[6]{0:T(512)(128)(4,1)S(1)}, u32[]{:S(2)}) copy-start(pred[6]{0:T(512)(128)(4,1)S(1)} %get-tuple-element.56) | copy-start | bytes 22
  78.4 155.3 %copy-start.58 = (pred[12]{0:T(512)(128)(4,1)}, pred[12]{0:T(512)(128)(4,1)S(1)}, u32[]{:S(2)}) copy-start(pred[12]{0:T(512)(128)(4,1)S(1)} %get-tuple-element.44) | copy-start | bytes 40
  78.4 155.3 %copy-start.62 = (pred[12]{0:T(512)(128)(4,1)}, pred[12]{0:T(512)(128)(4,1)S(1)}, u32[]{:S(2)}) copy-start(pred[12]{0:T(512)(128)(4,1)S(1)} %get-tuple-element.45) | copy-start | bytes 40
  79.0 154.7 %copy-start.60 = (pred[6]{0:T(512)(128)(4,1)}, pred[6]{0:T(512)(128)(4,1)S(1)}, u32[]{:S(2)}) copy-start(pred[6]{0:T(512)(128)(4,1)S(1)} %get-tuple-element.53) | copy-start | bytes 22
  302.4 84.9 %all-reduce.7.cloned.1.call-start = ((), (), s32[]{:S(2)}) async-start(), calls=%async_computation | async-start | bytes 786432 | tf_op jit(solution)/shard_map/psum | solution.py:126
  354.2 143.6 %all-reduce.13.cloned.1.call-start = ((), (), s32[]{:S(2)}) async-start(), calls=%async_computation.3 | async-start | bytes 1572864 | tf_op jit(solution)/shard_map/psum | solution.py:128
  367.6 19.6 %copy-start.48 = (pred[12,6]{0,1:T(8,128)(4,1)S(1)}, pred[12,6]{0,1:T(8,128)(4,1)}, u32[]{:S(2)}) copy-start(pred[12,6]{0,1:T(8,128)(4,1)} %get-tuple-element.36) | copy-start | bytes 220
  367.6 19.6 %copy-start.49 = (pred[12,6]{0,1:T(8,128)(4,1)S(1)}, pred[12,6]{0,1:T(8,128)(4,1)}, u32[]{:S(2)}) copy-start(pred[12,6]{0,1:T(8,128)(4,1)} %get-tuple-element.37) | copy-start | bytes 220
  367.6 19.6 %copy-start.65 = (pred[6]{0:T(512)(128)(4,1)S(1)}, pred[6]{0:T(512)(128)(4,1)}, u32[]{:S(2)}) copy-start(pred[6]{0:T(512)(128)(4,1)} %copy-done.64) | copy-start | bytes 22
  426.0 71.9 %copy-start.11 = (bf16[12,128,6,128]{3,1,2,0:T(8,128)(2,1)S(1)}, bf16[12,128,6,128]{3,1,2,0:T(8,128)(2,1)}, u32[]{:S(2)}) copy-start(bf16[12,128,6,128]{3,1,2,0:T(8,128)(2,1)} %get-tuple-element.27) | copy-start | bytes 7077892
  441.8 90.8 %copy-start.46 = (pred[12,6]{0,1:T(8,128)(4,1)S(1)}, pred[12,6]{0,1:T(8,128)(4,1)}, u32[]{:S(2)}) copy-start(pred[12,6]{0,1:T(8,128)(4,1)} %get-tuple-element.32) | copy-start | bytes 220
  441.8 90.8 %copy-start.47 = (pred[12,6]{0,1:T(8,128)(4,1)S(1)}, pred[12,6]{0,1:T(8,128)(4,1)}, u32[]{:S(2)}) copy-start(pred[12,6]{0,1:T(8,128)(4,1)} %get-tuple-element.33) | copy-start | bytes 220
  441.8 90.8 %all-reduce.11.cloned.1.call-start = ((), (), s32[]{:S(2)}) async-start(), calls=%async_computation.2 | async-start | bytes 786432 | tf_op jit(solution)/shard_map/psum | solution.py:126
  442.9 201.3 %all-reduce.17.cloned.1.call-start = ((), (), s32[]{:S(2)}) async-start(), calls=%async_computation.5 | async-start | bytes 1572864 | tf_op jit(solution)/shard_map/psum | solution.py:128
  532.7 13.2 %copy-start.63 = (pred[12]{0:T(512)(128)(4,1)S(1)}, pred[12]{0:T(512)(128)(4,1)}, u32[]{:S(2)}) copy-start(pred[12]{0:T(512)(128)(4,1)} %copy-done.62) | copy-start | bytes 40
  571.7 106.7 %all-reduce.15.cloned.1.call-start = ((), (), s32[]{:S(2)}) async-start(), calls=%async_computation.4 | async-start | bytes 786432 | tf_op jit(solution)/shard_map/psum | solution.py:126
  584.4 59.8 %copy-start.5 = (bf16[12,128,6,128]{3,1,2,0:T(8,128)(2,1)S(1)}, bf16[12,128,6,128]{3,1,2,0:T(8,128)(2,1)}, u32[]{:S(2)}) copy-start(bf16[12,128,6,128]{3,1,2,0:T(8,128)(2,1)} %get-tuple-element.24) | copy-start | bytes 7077892
  584.4 59.8 %copy-start.59 = (pred[12]{0:T(512)(128)(4,1)S(1)}, pred[12]{0:T(512)(128)(4,1)}, u32[]{:S(2)}) copy-start(pred[12]{0:T(512)(128)(4,1)} %copy-done.58) | copy-start | bytes 40
  590.6 87.8 %copy-start.45 = (pred[12,6]{0,1:T(8,128)(4,1)S(1)}, pred[12,6]{0,1:T(8,128)(4,1)}, u32[]{:S(2)}) copy-start(pred[12,6]{0,1:T(8,128)(4,1)} %get-tuple-element.35) | copy-start | bytes 220
  590.6 87.8 %copy-start.61 = (pred[6]{0:T(512)(128)(4,1)S(1)}, pred[6]{0:T(512)(128)(4,1)}, u32[]{:S(2)}) copy-start(pred[6]{0:T(512)(128)(4,1)} %copy-done.60) | copy-start | bytes 22
  697.7 14.8 %copy-start.1 = (f32[12,128,128]{2,1,0:T(8,128)S(1)}, f32[12,128,128]{2,1,0:T(8,128)}, u32[]{:S(2)}) copy-start(f32[12,128,128]{2,1,0:T(8,128)} %param.24) | copy-start | bytes 2359300
  (62 other events, 431.7 us)
Sparse Core Ops, SparseCore 0:
  272.6 75.0 all-reduce.8
  354.4 32.8 all-reduce.6
  422.7 75.0 all-reduce.12
  500.7 31.9 all-reduce.10
  569.1 75.0 all-reduce.16
  646.4 31.9 all-reduce.14
where the time goes:
time: 731 us; the launch traced here: 720 us
  waiting for transfers between devices  320 us (44%)
  local copies, waits for them, and re-layouts  194 us (27%)
  matrix products  112 us (15%)
  other arithmetic  70 us (10%)
  between operations  16 us (2%)
  starting transfers between devices  8.39 us (1%)
    ppermute x2, waiting for transfers between devices, padded(): before = lax.ppermute(last, axis, up)  137 us
    psum x3, waiting for transfers between devices, body(): front_l = lax.psum(picked, 'col')  109 us
    psum x3, waiting for transfers between devices, body(): front_r = lax.psum(new_r, 'row')  72.6 us
    unnamed x176, local copies, waits for them, and re-layouts  49.8 us
    dot_general x27, matrix products, product(): jnp.einsum('bij,bjk->bik', left, right, precision=lax.Precision.HIGHEST)  30.8 us
    dot_general x3, matrix products, body(): jnp.einsum('apbq,bqs->apbs', panel_a.astype(jnp.float32), front_r, precis...  29.1 us
    slice x4, local copies, waits for them, and re-layouts, body(): picked_ad = jnp.take(near_ad[:, :, :, :, 1 + offset, :], slot_cols, axis=3)  26.2 us
    dot_general x3, matrix products, body(): jnp.einsum('apbq,bqs->apbs', panel_d.astype(jnp.float32), front_r, precis...  24.4 us
  transfers between devices with their start and end apart: 10, of which 7 were waited for; matrix products, arithmetic and copies ran while one was open for 35% of the time, Pallas kernels for 0%

commit v1 on v0

--- a/solution.py
+++ b/solution.py
@@ -125,7 +125,7 @@
         l_slot = jnp.clip(cols_clip // count_cols, 0, cols_dev - 1)
         front_r = lax.psum(new_r, "row")
         picked = jnp.where((cols_clip % count_cols == this_col)[:, None, None], new_l[l_slot], 0.0)
-        front_l = lax.psum(picked, "col")
+        front_l = jnp.sum(lax.all_gather(picked, "col"), axis=0)
         front_r = jnp.where(col_valid[:, None, None], front_r, 0.0)
         front_l = jnp.where(row_valid[:, None, None], front_l, 0.0)
         mask_a = (block_rows[:, None] < front_rows[None, :]) & col_valid[None, :]

time: 731 us -> 800 us (1.094)
  waiting for transfers between devices: 320 us -> 380 us
    ppermute x2, waiting for transfers between devices: 137 us -> 256 us  [padded(): before = lax.ppermute(last, axis, up)]
    psum x3 -> x0, waiting for transfers between devices: 109 us -> none  [body(): front_l = lax.psum(picked, 'col')]
    all_gather x0 -> x3, waiting for transfers between devices: none -> 106 us  [body(): front_l = jnp.sum(lax.all_gather(picked, 'col'), axis=0)]
    psum x3, waiting for transfers between devices: 72.6 us -> 14.1 us  [body(): front_r = lax.psum(new_r, 'row')]
    reduce_sum x0 -> x3, other arithmetic: none -> 10.9 us  [body(): front_l = jnp.sum(lax.all_gather(picked, 'col'), axis=0)]
    unnamed x176 -> x144, local copies, waits for them, and re-layouts: 49.8 us -> 51 us
  transfers between devices with their start and end apart: 10 -> 10, of which waited for: 7 -> 7; matrix products, arithmetic and copies ran while one was open for 35% -> 28% of each run, Pallas kernels for 0% -> 0%
where the time goes in v1:
time: 800 us; the launch traced here: 790 us
  waiting for transfers between devices  380 us (48%)
  local copies, waits for them, and re-layouts  192 us (24%)
  matrix products  118 us (15%)
  other arithmetic  75.2 us (9%)
  between operations  16.7 us (2%)
  starting transfers between devices  8.39 us (1%)
    ppermute x2, waiting for transfers between devices, padded(): before = lax.ppermute(last, axis, up)  256 us
    all_gather x3, waiting for transfers between devices, body(): front_l = jnp.sum(lax.all_gather(picked, 'col'), axis=0)  106 us
    unnamed x144, local copies, waits for them, and re-layouts  51 us
    dot_general x27, matrix products, product(): jnp.einsum('bij,bjk->bik', left, right, precision=lax.Precision.HIGHEST)  34.5 us
    dot_general x3, matrix products, body(): jnp.einsum('apbq,bqs->apbs', panel_d.astype(jnp.float32), front_r, precis...  30.2 us
    dot_general x3, matrix products, body(): jnp.einsum('apbq,bqs->apbs', panel_a.astype(jnp.float32), front_r, precis...  29 us
    slice x4, local copies, waits for them, and re-layouts, body(): picked_ad = jnp.take(near_ad[:, :, :, :, 1 + offset, :], slot_cols, axis=3)  26.1 us
    gather x3, local copies, waits for them, and re-layouts, body(): picked_be = jnp.take(near_be[:, :, 1 - offset, :, :, :], slot_rows, axis=1)  18 us
  transfers between devices with their start and end apart: 10, of which 7 were waited for; matrix products, arithmetic and copies ran while one was open for 28% of the time, Pallas kernels for 0%

profile of v1, /device:TPU:0, one launch (start us, length us, event | category | flops | bytes accessed | tf_op | source)
XLA Modules:
  0.0 790.5 jit_solution(7011367712666069996)
XLA Ops:
  43.5 181.8 %collective-permute-done = bf16[2,12,128,6,128]{2,4,3,1,0:T(8,128)(2,1)} collective-permute-done((bf16[2,12,128,6,128]{2,4,3,1,0:T(8,128)(2,1)}, bf16[2,12,128,6,128]{2,4,3,1,0:T(8,128)(2,1)}, u32[]{:S(2)}, u32[]{:S(2)}) %collective-permute-start) | collective-permute-done | bytes 4718624 | tf_op jit(solution)/shard_map/ppermute | solution.py:18
  227.4 6.9 pad_maximum_fusion
  234.3 6.2 fusion.108
  240.5 6.6 copy.131
  247.1 5.9 gather_fusion.27
  279.7 6.3 copy.136
  286.0 6.1 copy.139
  305.5 74.1 %collective-permute-done.2 = bf16[2,12,128,6,128]{4,2,3,1,0:T(8,128)(2,1)} collective-permute-done((bf16[2,12,128,6,128]{4,2,3,1,0:T(8,128)(2,1)}, bf16[2,12,128,6,128]{4,2,3,1,0:T(8,128)(2,1)}, u32[]{:S(2)}, u32[]{:S(2)}) %collective-permute-start.2) | collective-permute-done | bytes 4718624 | tf_op jit(solution)/shard_map/ppermute | solution.py:18
  380.9 6.9 pad_maximum_fusion.1
  387.8 6.2 slice_bitcast_fusion
  394.0 6.0 gather_fusion.28
  412.3 6.6 copy.141
  418.9 5.9 gather_fusion.29
  441.0 5.4 fusion.29
  450.5 14.1 %all-reduce.4.cloned.1.call-done = f32[6,128,128]{2,1,0:T(8,128)} async-done(((f32[6,128,128]{2,1,0:T(8,128)}), f32[6,128,128]{2,1,0:T(8,128)}) %all-reduce.4.cloned.1.call-update) | async-done | bytes 393232 | tf_op jit(solution)/shard_map/psum | solution.py:126
  464.6 10.1 %fusion.11 = f32[12,128,6,128]{1,3,0,2:T(8,128)} fusion(f32[12,128,6,128]{1,3,0,2:T(8,128)} %copy.136, f32[12,128,6,128]{1,3,0,2:T(8,128)} %fusion.31, pred[12,6]{0,1:T(8,128)(4,1)S(1)} %copy-done.41, pred[12,6]{0,1:T(8,128)(4,1)S(1)} %copy-done.42, f32[6,128,128]{2,1,0:T(8,128)} %all-reduce.4.cloned.1.call-done, pred[6]{0:T(512)(128)(4,1)S(1)} %copy-done.59, ...), kind=kOutput, calls=%fused_computation.57 | convolution fusion | flops 1816756224 | bytes 16908438 | tf_op jit(solution)/shard_map/apbq,bqs->apbs/dot_general | solution.py:132
  477.7 10.0 %fusion.9 = f32[12,128,6,128]{1,3,0,2:T(8,128)} fusion(f32[12,128,6,128]{1,3,0,2:T(8,128)} %copy.139, f32[12,128,6,128]{1,3,0,2:T(8,128)} %fusion.29, pred[12,6]{0,1:T(8,128)(4,1)S(1)} %copy-done.41, pred[12,6]{0,1:T(8,128)(4,1)S(1)} %copy-done.42, bf16[2,12,128,6,128]{4,2,1,3,0:T(8,128)(2,1)} %copy-done.3, f32[6,128,128]{2,1,0:T(8,128)S(1)} %copy-done.33, ...), kind=kOutput, calls=%fused_computation.54 | convolution fusion | flops 1816756224 | bytes 16908438 | tf_op jit(solution)/shard_map/apbq,bqs->apbs/dot_general | solution.py:135
  508.3 6.1 gather_fusion.30
  521.2 6.6 copy.154
  527.8 5.9 gather_fusion.31
  549.6 49.4 %all-gather.6.cloned.1.call-done = f32[8,12,128,128]{3,2,1,0:T(8,128)} async-done(((f32[1,12,128,128]{3,2,1,0:T(8,128)}), f32[8,12,128,128]{3,2,1,0:T(8,128)}) %all-gather.6.cloned.1.call-update) | async-done | bytes 6291472 | tf_op jit(solution)/shard_map/all_gather | solution.py:128
  610.9 10.1 %fusion.7 = f32[12,128,6,128]{1,3,0,2:T(8,128)} fusion(f32[12,128,6,128]{1,3,0,2:T(8,128)} %fusion.11, f32[12,128,6,128]{1,3,0,2:T(8,128)} %fusion.27, pred[12,6]{0,1:T(8,128)(4,1)S(1)} %copy-done.40, pred[12,6]{0,1:T(8,128)(4,1)S(1)} %copy-done.39, f32[6,128,128]{2,1,0:T(8,128)} %all-reduce.6.cloned.1.call-done, pred[6]{0:T(512)(128)(4,1)S(1)} %copy-done.44, ...), kind=kOutput, calls=%fused_computation.51 | convolution fusion | flops 1816756224 | bytes 16908438 | tf_op jit(solution)/shard_map/apbq,bqs->apbs/dot_general | solution.py:132
  624.0 10.1 %fusion.5 = f32[12,128,6,128]{1,3,0,2:T(8,128)} fusion(f32[12,128,6,128]{1,3,0,2:T(8,128)} %fusion.9, f32[12,128,6,128]{1,3,0,2:T(8,128)} %fusion.25, pred[12,6]{0,1:T(8,128)(4,1)S(1)} %copy-done.40, pred[12,6]{0,1:T(8,128)(4,1)S(1)} %copy-done.39, bf16[2,12,128,6,128]{4,2,1,3,0:T(8,128)(2,1)} %copy-done.4, f32[6,128,128]{2,1,0:T(8,128)S(1)} %copy-done.35, ...), kind=kOutput, calls=%fused_computation.48 | convolution fusion | flops 1816756224 | bytes 16908438 | tf_op jit(solution)/shard_map/apbq,bqs->apbs/dot_general | solution.py:135
  646.6 5.8 gather_fusion.32
  665.9 6.7 select_add_fusion
  672.6 6.1 copy.175
  678.7 6.0 copy.176
  684.8 56.8 %all-gather.8.cloned.1.call-done = f32[8,12,128,128]{3,2,1,0:T(8,128)} async-done(((f32[1,12,128,128]{3,2,1,0:T(8,128)}), f32[8,12,128,128]{3,2,1,0:T(8,128)}) %all-gather.8.cloned.1.call-update) | async-done | bytes 6291472 | tf_op jit(solution)/shard_map/all_gather | solution.py:128
  749.0 10.1 %fusion.1 = f32[12,128,6,128]{1,3,0,2:T(8,128)} fusion(f32[12,128,6,128]{1,3,0,2:T(8,128)} %fusion.5, f32[12,128,6,128]{1,3,0,2:T(8,128)} %fusion.21, pred[12,6]{0,1:T(8,128)(4,1)S(1)} %copy-done.38, pred[12,6]{0,1:T(8,128)(4,1)S(1)} %copy-done.37, bf16[2,12,128,6,128]{4,2,1,3,0:T(8,128)(2,1)} %copy-done.2, ...), kind=kOutput, calls=%fused_computation.42 | convolution fusion | flops 1816756224 | bytes 16908438 | tf_op jit(solution)/shard_map/apbq,bqs->apbs/dot_general | solution.py:135
  759.0 6.4 copy.174
  768.1 8.7 %fusion.3 = f32[12,128,6,128]{1,3,0,2:T(8,128)} fusion(f32[12,128,6,128]{1,3,0,2:T(8,128)} %fusion.7, f32[12,128,6,128]{1,3,0,2:T(8,128)S(1)} %fusion.23, pred[12,6]{0,1:T(8,128)(4,1)S(1)} %copy-done.38, pred[12,6]{0,1:T(8,128)(4,1)S(1)} %copy-done.37, f32[6,128,128]{2,1,0:T(8,128)S(1)} %copy-done.34, pred[6]{0:T(512)(128)(4,1)S(1)} %copy-done.54, ...), kind=kOutput, calls=%fused_computation.45 | convolution fusion | flops 1816756224 | bytes 16908438 | tf_op jit(solution)/shard_map/apbq,bqs->apbs/dot_general | solution.py:132
  776.9 6.0 copy.173
  (290 shorter events, 207.6 us)
Async XLA Ops:
  8.0 25.7 %copy-start = (f32[12,128,128]{2,1,0:T(8,128)S(1)}, f32[12,128,128]{2,1,0:T(8,128)}, u32[]{:S(2)}) copy-start(f32[12,128,128]{2,1,0:T(8,128)} %param.24) | copy-start | bytes 2359300
  8.0 428.7 %all-gather.4.cloned.1.call-start = ((), (), s32[]{:S(2)}) async-start(), calls=%async_computation.1 | async-start | bytes 7077888 | tf_op jit(solution)/shard_map/all_gather | solution.py:128
  15.4 22.0 %copy-start.36 = (f32[12,128]{1,0:T(8,128)S(1)}, f32[12,128]{1,0:T(8,128)}, u32[]{:S(2)}) copy-start(f32[12,128]{1,0:T(8,128)} %param.27) | copy-start | bytes 18436
  19.7 205.5 %collective-permute-start = (bf16[2,12,128,6,128]{2,4,3,1,0:T(8,128)(2,1)}, bf16[2,12,128,6,128]{2,4,3,1,0:T(8,128)(2,1)}, u32[]{:S(2)}, u32[]{:S(2)}) collective-permute-start(bf16[2,12,128,6,128]{2,4,3,1,0:T(8,128)(2,1)} %pad_maximum_fusion.2), channel_id=1, source_target_pairs={{0,1},{1,2},{2,3},{3,4},{4,5},{5,6},{6,7},{7,0},{8,9},{9,10},{10,1... | collective-permute-start | bytes 14155784 | tf_op jit(solution)/shard_map/ppermute | solution.py:18
  22.7 204.7 %collective-permute-start.1 = (bf16[2,12,128,6,128]{2,4,3,1,0:T(8,128)(2,1)}, bf16[2,12,128,6,128]{2,4,3,1,0:T(8,128)(2,1)}, u32[]{:S(2)}, u32[]{:S(2)}) collective-permute-start(bf16[2,12,128,6,128]{2,4,3,1,0:T(8,128)(2,1)} %pad_maximum_fusion.2), channel_id=1, source_target_pairs={{1,0},{2,1},{3,2},{4,3},{5,4},{6,5},{7,6},{0,7},{9,8},{10,9},{11,1... | collective-permute-start | bytes 14155784 | tf_op jit(solution)/shard_map/ppermute | solution.py:19
  29.2 233.0 %copy-start.14 = (f32[6,128,128]{2,1,0:T(8,128)}, f32[6,128,128]{2,1,0:T(8,128)S(1)}, u32[]{:S(2)}) copy-start(f32[6,128,128]{2,1,0:T(8,128)S(1)} %gather_fusion.1) | copy-start | bytes 1179652
  42.3 225.9 %copy-start.45 = (pred[6]{0:T(512)(128)(4,1)}, pred[6]{0:T(512)(128)(4,1)S(1)}, u32[]{:S(2)}) copy-start(pred[6]{0:T(512)(128)(4,1)S(1)} %get-tuple-element.59) | copy-start | bytes 22
  277.5 102.2 %collective-permute-start.2 = (bf16[2,12,128,6,128]{4,2,3,1,0:T(8,128)(2,1)}, bf16[2,12,128,6,128]{4,2,3,1,0:T(8,128)(2,1)}, u32[]{:S(2)}, u32[]{:S(2)}) collective-permute-start(bf16[2,12,128,6,128]{4,2,3,1,0:T(8,128)(2,1)} %pad_maximum_fusion.3), channel_id=1, source_target_pairs={{0,8},{8,16},{16,24},{24,0},{1,9},{9,17},{17,25},{25,1},{2,10},{10... | collective-permute-start | bytes 14155784 | tf_op jit(solution)/shard_map/ppermute | solution.py:18
  277.5 103.4 %collective-permute-start.3 = (bf16[2,12,128,6,128]{4,2,3,1,0:T(8,128)(2,1)}, bf16[2,12,128,6,128]{4,2,3,1,0:T(8,128)(2,1)}, u32[]{:S(2)}, u32[]{:S(2)}) collective-permute-start(bf16[2,12,128,6,128]{4,2,3,1,0:T(8,128)(2,1)} %pad_maximum_fusion.3), channel_id=1, source_target_pairs={{8,0},{16,8},{24,16},{0,24},{9,1},{17,9},{25,17},{1,25},{10,2},{18... | collective-permute-start | bytes 14155784 | tf_op jit(solution)/shard_map/ppermute | solution.py:19
  301.2 78.5 %copy-start.60 = (pred[12]{0:T(512)(128)(4,1)}, pred[12]{0:T(512)(128)(4,1)S(1)}, u32[]{:S(2)}) copy-start(pred[12]{0:T(512)(128)(4,1)S(1)} %compare_and_fusion.18) | copy-start | bytes 40
  301.2 78.5 %copy-start.58 = (pred[6]{0:T(512)(128)(4,1)}, pred[6]{0:T(512)(128)(4,1)S(1)}, u32[]{:S(2)}) copy-start(pred[6]{0:T(512)(128)(4,1)S(1)} %compare_and_fusion.20) | copy-start | bytes 22
  302.4 77.3 %copy-start.43 = (pred[6]{0:T(512)(128)(4,1)}, pred[6]{0:T(512)(128)(4,1)S(1)}, u32[]{:S(2)}) copy-start(pred[6]{0:T(512)(128)(4,1)S(1)} %get-tuple-element.61) | copy-start | bytes 22
  302.5 77.2 %copy-start.51 = (pred[12]{0:T(512)(128)(4,1)}, pred[12]{0:T(512)(128)(4,1)S(1)}, u32[]{:S(2)}) copy-start(pred[12]{0:T(512)(128)(4,1)S(1)} %get-tuple-element.48) | copy-start | bytes 40
  302.5 77.2 %copy-start.55 = (pred[12]{0:T(512)(128)(4,1)}, pred[12]{0:T(512)(128)(4,1)S(1)}, u32[]{:S(2)}) copy-start(pred[12]{0:T(512)(128)(4,1)S(1)} %get-tuple-element.49) | copy-start | bytes 40
  303.0 76.7 %copy-start.53 = (pred[6]{0:T(512)(128)(4,1)}, pred[6]{0:T(512)(128)(4,1)S(1)}, u32[]{:S(2)}) copy-start(pred[6]{0:T(512)(128)(4,1)S(1)} %get-tuple-element.57) | copy-start | bytes 22
  412.3 52.3 %all-reduce.4.cloned.1.call-start = ((), (), s32[]{:S(2)}) async-start(), calls=%async_computation | async-start | bytes 786432 | tf_op jit(solution)/shard_map/psum | solution.py:126
  431.5 167.6 %all-gather.6.cloned.1.call-start = ((), (), s32[]{:S(2)}) async-start(), calls=%async_computation.3 | async-start | bytes 7077888 | tf_op jit(solution)/shard_map/all_gather | solution.py:128
  446.3 18.3 %copy-start.41 = (pred[12,6]{0,1:T(8,128)(4,1)S(1)}, pred[12,6]{0,1:T(8,128)(4,1)}, u32[]{:S(2)}) copy-start(pred[12,6]{0,1:T(8,128)(4,1)} %get-tuple-element.40) | copy-start | bytes 220
  446.3 18.3 %copy-start.42 = (pred[12,6]{0,1:T(8,128)(4,1)S(1)}, pred[12,6]{0,1:T(8,128)(4,1)}, u32[]{:S(2)}) copy-start(pred[12,6]{0,1:T(8,128)(4,1)} %get-tuple-element.41) | copy-start | bytes 220
  446.3 18.3 %copy-start.59 = (pred[6]{0:T(512)(128)(4,1)S(1)}, pred[6]{0:T(512)(128)(4,1)}, u32[]{:S(2)}) copy-start(pred[6]{0:T(512)(128)(4,1)} %copy-done.58) | copy-start | bytes 22
  477.7 15.2 %copy-start.19 = (f32[6,128,128]{2,1,0:T(8,128)S(1)}, f32[6,128,128]{2,1,0:T(8,128)}, u32[]{:S(2)}) copy-start(f32[6,128,128]{2,1,0:T(8,128)} %param.28) | copy-start | bytes 1179652
  477.7 16.0 %copy-start.29 = (f32[6,128,128]{2,1,0:T(8,128)S(1)}, f32[6,128,128]{2,1,0:T(8,128)}, u32[]{:S(2)}) copy-start(f32[6,128,128]{2,1,0:T(8,128)} %gather_fusion.12) | copy-start | bytes 1179652
  497.7 16.7 %copy-start.10 = (f32[6,128,128]{2,1,0:T(8,128)}, f32[6,128,128]{2,1,0:T(8,128)S(1)}, u32[]{:S(2)}) copy-start(f32[6,128,128]{2,1,0:T(8,128)S(1)} %get-tuple-element.44) | copy-start | bytes 1179652
  547.1 55.3 %copy-start.56 = (pred[12]{0:T(512)(128)(4,1)S(1)}, pred[12]{0:T(512)(128)(4,1)}, u32[]{:S(2)}) copy-start(pred[12]{0:T(512)(128)(4,1)} %copy-done.55) | copy-start | bytes 40
  549.0 61.9 %all-reduce.6.cloned.1.call-start = ((), (), s32[]{:S(2)}) async-start(), calls=%async_computation.2 | async-start | bytes 786432 | tf_op jit(solution)/shard_map/psum | solution.py:126
  549.5 192.0 %all-gather.8.cloned.1.call-start = ((), (), s32[]{:S(2)}) async-start(), calls=%async_computation.5 | async-start | bytes 7077888 | tf_op jit(solution)/shard_map/all_gather | solution.py:128
  624.0 13.1 %copy-start.32 = (f32[6,128,128]{2,1,0:T(8,128)S(1)}, f32[6,128,128]{2,1,0:T(8,128)}, u32[]{:S(2)}) copy-start(f32[6,128,128]{2,1,0:T(8,128)} %fusion.117) | copy-start | bytes 1179652
  624.0 14.1 %copy-start.20 = (f32[6,128,128]{2,1,0:T(8,128)S(1)}, f32[6,128,128]{2,1,0:T(8,128)}, u32[]{:S(2)}) copy-start(f32[6,128,128]{2,1,0:T(8,128)} %param.28) | copy-start | bytes 1179652
  624.0 14.9 %copy-start.31 = (f32[6,128,128]{2,1,0:T(8,128)S(1)}, f32[6,128,128]{2,1,0:T(8,128)}, u32[]{:S(2)}) copy-start(f32[6,128,128]{2,1,0:T(8,128)} %gather_fusion.21) | copy-start | bytes 1179652
  664.9 84.1 %all-reduce.8.cloned.1.call-start = ((), (), s32[]{:S(2)}) async-start(), calls=%async_computation.4 | async-start | bytes 786432 | tf_op jit(solution)/shard_map/psum | solution.py:126
  684.7 60.2 %copy-start.52 = (pred[12]{0:T(512)(128)(4,1)S(1)}, pred[12]{0:T(512)(128)(4,1)}, u32[]{:S(2)}) copy-start(pred[12]{0:T(512)(128)(4,1)} %copy-done.51) | copy-start | bytes 40
  768.1 14.8 %copy-start.1 = (f32[12,128,128]{2,1,0:T(8,128)S(1)}, f32[12,128,128]{2,1,0:T(8,128)}, u32[]{:S(2)}) copy-start(f32[12,128,128]{2,1,0:T(8,128)} %param.24) | copy-start | bytes 2359300
  (46 other events, 279.6 us)
Sparse Core Ops, SparseCore 0:
  273.3 98.7 all-gather.3
  500.3 98.6 all-gather.5
  644.7 96.8 all-gather.7
Sparse Core Ops, SparseCore 1:
  431.6 33.0 all-reduce.3
  552.4 32.7 all-reduce.5
  684.9 31.1 all-reduce.7
